TPU v7x, 32 devices: a whole 2x2x4 slice. The times are simulated.
32 devices in a mesh: row: 4 (over y, x), col: 8 (over z, core).
Axes of the slice: x: 2, y: 2, z: 4, core: 2. Of those that a mesh axis runs over, the one named last changes fastest.
Arguments:
- points: bfloat16 [10240, 64], P(('row', 'col')), may hold values from -5 to 5
- start_vectors: bfloat16 [10240, 32], P(('row', 'col')), may hold values from -12 to 12
Outputs:
- basis: float32 [10240, 32], P(('row', 'col'))
All inputs are finite; a program needn't handle non-finite values.
Results may differ from a plain program's by a relative error of at most 0.007.
Values may be sent and summed in bfloat16 or wider, within the bound.
A program may use at most 64 MiB of HBM per device.

v0:
```python
import functools

import jax
import jax.numpy as jnp
from jax import lax
from jax.experimental import pallas as pl
from jax.experimental.pallas import tpu as pltpu
from jax.sharding import PartitionSpec as P

KERNEL_SCALE = 5.12
LOG2E = 1.4426950408889634
MESH = pl.DeviceIdType.MESH
HIGHEST = lax.Precision.HIGHEST
LANES = 128


def packing(rows):
    for stacks in (4, 2, 1):
        if rows % (16 * stacks) == 0:
            return stacks
    raise ValueError(rows)


def square_side(count):
    side = 1
    while side * side < count:
        side += 1
    return side if side * side == count else count


def upright(value):
    return value.astype(jnp.float32).T.astype(value.dtype)


def width(stacks, lanes):
    return -(-stacks * lanes // LANES) * LANES


def side_by_side(value, stacks):
    rows, lanes = value.shape
    high = rows // stacks
    pieces = [value[s * high : (s + 1) * high] for s in range(stacks)]
    spare = width(stacks, lanes) - stacks * lanes
    if spare:
        pieces.append(jnp.zeros((high, spare), value.dtype))
    return jnp.concatenate(pieces, axis=1)


def inverse_factor(gram):
    size = gram.shape[0]
    down = lax.broadcasted_iota(jnp.int32, (size, size), 0)
    across = lax.broadcasted_iota(jnp.int32, (size, size), 1)
    unit = (down == across).astype(jnp.float32)
    work = jnp.concatenate([gram, unit], axis=1)
    below = lax.broadcasted_iota(jnp.int32, work.shape, 0)
    panel = 8
    for first in range(0, size, panel):
        columns = [jnp.broadcast_to(work[:, k : k + 1], work.shape) for k in range(first, first + panel)]
        for m in range(panel):
            k = first + m
            factor = jnp.where(below > k, columns[m] * (1.0 / columns[m][k : k + 1]), 0.0)
            work = work - factor * work[k : k + 1]
            for later in range(m + 1, panel):
                columns[later] = columns[later] - factor * columns[later][k : k + 1]
    pivots = jnp.sum(work[:, :size] * unit, axis=1, keepdims=True)
    return work[:, size:] * lax.rsqrt(pivots)


def kernel(nrow, ncol, total, pts_ref, vec_ref, out_ref, gp, gv, gs, aff, acc,
           gram_col, gram_row, sems_p, sems_v, sems_s, sems_g):
    row, col = lax.axis_index("row"), lax.axis_index("col")
    nz = ncol // 2
    z, core = col // 2, col % 2
    sibling = z * 2 + (1 - core)
    features, rows = pts_ref.shape
    vectors = vec_ref.shape[0]
    side = square_side(nrow)
    high_row, low_row = row // side, row % side
    stacks = packing(rows)
    high = rows // stacks
    per_tile = max(1, LANES // features)

    def row_at(j):
        return lax.rem(high_row + j // side, nrow // side) * side + lax.rem(low_row + j % side, side)

    straight = [j for j in range(1, nrow) if j // side == 0 or j % side == 0]
    oblique = [j for j in range(1, nrow) if j // side and j % side]

    def col_at(k):
        return lax.rem(z + k, nz) * 2 + core

    def view(buf, r, c):
        return buf.at[r, pl.ds(pl.multiple_of(c * high, high), high)]

    def block(buf, r, c, send, recv, to_row, to_col):
        return pltpu.make_async_remote_copy(
            src_ref=view(buf, r, c), dst_ref=view(buf, r, c), send_sem=send, recv_sem=recv.at[r, c],
            device_id=(to_row, to_col), device_id_type=MESH,
        )

    def arrived(gather, r, c):
        buf, recv, along, spread, pair, onward, routed = gather
        block(buf, r, c, pair.at[0, 0], recv, row, sibling).wait_recv()

    def hand_over(gather, j, k):
        buf, recv, along, spread, pair, onward, routed = gather
        block(buf, row_at(j), col_at(k), pair.at[j, k], recv, row, sibling).start()

    def send_plane(gather, k):
        buf, recv, along, spread, pair, onward, routed = gather
        for j in straight + (oblique if routed else []):
            block(buf, row, col_at(k), spread.at[k, j], recv, row_at(j), col).start()
        hand_over(gather, 0, k)

    def relays(gather, j, k):
        buf, recv, along, spread, pair, onward, routed = gather
        copies = []
        if routed:
            targets = []
        elif j // side == 0 and k % 2 == 0:
            targets = [d * side for d in range(1, nrow // side)]
        elif j % side == 0 and k % 2 == 1:
            targets = range(1, side)
        else:
            targets = []
        return [
            block(buf, row_at(j), col_at(k), onward.at[j, k, i], recv, row_at(t), col)
            for i, t in enumerate(targets)
        ]

    def relay(gather, k):
        for j in straight:
            arrived(gather, row_at(j), col_at(k))
            for copy in relays(gather, j, k):
                copy.start()
            hand_over(gather, j, k)

    def send_own(gather):
        buf, recv, along, spread, pair, onward, routed = gather
        for k in range(1, nz):
            block(buf, row, col, along.at[k - 1], recv, row, col_at(k)).start()
        send_plane(gather, 0)

    def pass_on(gather, k):
        arrived(gather, row, col_at(k))
        send_plane(gather, k)

    def hand_over_row(gather, j):
        for k in range(nz):
            arrived(gather, row_at(j), col_at(k))
            hand_over(gather, j, k)

    def sibling_row(gather, j):
        for k in range(nz):
            arrived(gather, row_at(j), lax.rem(z + k, nz) * 2 + (1 - core))

    def drain(gather):
        buf, recv, along, spread, pair, onward, routed = gather
        for k in range(1, nz):
            block(buf, row, col, along.at[k - 1], recv, row, col_at(k)).wait_send()
        for k in range(nz):
            for j in straight + (oblique if routed else []):
                block(buf, row, col_at(k), spread.at[k, j], recv, row_at(j), col).wait_send()
                for copy in relays(gather, j, k):
                    copy.wait_send()
            for j in range(nrow):
                block(buf, row_at(j), col_at(k), pair.at[j, k], recv, row, sibling).wait_send()

    points = (gp,) + tuple(sems_p) + (False,)
    start = (gv,) + tuple(sems_v) + (False,)
    middle = (gs,) + tuple(sems_s) + (True,)

    barrier = pltpu.get_barrier_semaphore()
    for j in range(1, nrow):
        pl.semaphore_signal(barrier, inc=1, device_id=(row_at(j), col), device_id_type=MESH)
    for k in range(1, ncol):
        pl.semaphore_signal(barrier, inc=1, device_id=(row, lax.rem(col + k, ncol)), device_id_type=MESH)

    own = pl.ds(pl.multiple_of(col * high, high), high)
    x = upright(pts_ref[...])
    gp[row, own, :] = side_by_side(x, stacks)
    gv[row, own, :] = side_by_side(upright(vec_ref[...]), stacks)
    pl.semaphore_wait(barrier, nrow + ncol - 2)

    send_own(points)
    send_own(start)

    rate = -KERNEL_SCALE / features * LOG2E
    xf = x.astype(jnp.float32)
    here = jnp.sum(xf * xf, axis=1, keepdims=True) * rate
    blank = jnp.zeros_like(x)
    left = []
    for s in range(per_tile):
        parts = [x if s == t else blank for t in range(per_tile)]
        left.append(jnp.concatenate(parts, axis=1))
    lane = lax.broadcasted_iota(jnp.int32, (8 * per_tile, LANES), 1)
    down = lax.broadcasted_iota(jnp.int32, (8 * per_tile, LANES), 0)
    picks = (lane // features == down // 8).astype(jnp.bfloat16)
    contract = (((1,), (1,)), ((), ()))

    def weights(r):
        for s in range(stacks):
            tile, part = s // per_tile, s % per_tile
            right = gp[r, :, tile * LANES : (tile + 1) * LANES]
            if part == 0:
                wide = right.astype(jnp.float32)
                square = wide * wide
                upper = square.astype(jnp.bfloat16)
                lower = (square - upper.astype(jnp.float32)).astype(jnp.bfloat16)
                there = (
                    lax.dot_general(picks, upper, contract, preferred_element_type=jnp.float32)
                    + lax.dot_general(picks, lower, contract, preferred_element_type=jnp.float32)
                ) * rate
            cross = lax.dot_general(left[part], right, contract, preferred_element_type=jnp.float32)
            power = (cross * (-2.0 * rate) + there[8 * part : 8 * part + 1]) + here
            aff[r, s] = jnp.exp2(power).astype(jnp.bfloat16)

    for k in range(1, nz):
        pass_on(points, k)
        pass_on(start, k)
        relay(points, k - 1)
    relay(points, nz - 1)
    sibling_row(points, 0)
    weights(row)
    for k in range(nz):
        relay(start, k)
    for j in straight:
        sibling_row(points, j)
        weights(row_at(j))
        if j == straight[0]:
            for o in oblique:
                hand_over_row(points, o)
    for j in oblique:
        sibling_row(points, j)
        weights(row_at(j))

    span = gv.shape[2]
    ones = jnp.ones((ncol * high, LANES), jnp.bfloat16)
    acc[...] = jnp.zeros_like(acc)

    def first_row(j):
        sibling_row(start, j)
        r = row_at(j)
        panel = jnp.concatenate([gv[r], ones], axis=1)
        for s in range(stacks):
            acc[s] += jnp.dot(aff[r, s], panel, preferred_element_type=jnp.float32)

    for j in oblique:
        hand_over_row(start, j)
    for j in [0] + straight:
        first_row(j)
    for j in oblique:
        first_row(j)

    product = sum(acc[s][:, s * vectors : (s + 1) * vectors] for s in range(stacks))
    degree = sum(acc[s][:, span : span + vectors] for s in range(stacks))
    scaled = product / degree
    gs[row, own, :] = side_by_side(scaled.astype(jnp.bfloat16), stacks)
    send_own(middle)

    folds = LANES // vectors
    tall = vectors // folds

    def gram_send(step, value):
        part = jnp.dot(value.T, value, precision=HIGHEST, preferred_element_type=jnp.float32) * (1.0 / total)
        gram_col[step, col] = jnp.concatenate([part[f * tall : (f + 1) * tall] for f in range(folds)], axis=1)
        for k in range(1, ncol):
            gram_copy(gram_col, step, col, k - 1, row, lax.rem(col + k, ncol), 0).start()

    def gram_copy(buf, step, slot, k, to_row, to_col, axis):
        return pltpu.make_async_remote_copy(
            src_ref=buf.at[step, slot], dst_ref=buf.at[step, slot],
            send_sem=sems_g[2 * axis].at[step, k], recv_sem=sems_g[2 * axis + 1].at[step, slot],
            device_id=(to_row, to_col), device_id_type=MESH,
        )

    def gram_across(step):
        for k in range(1, ncol):
            slot = lax.rem(col + k, ncol)
            gram_copy(gram_col, step, slot, k - 1, row, slot, 0).wait_recv()
        gram_row[step, row] = sum(gram_col[step, c] for c in range(ncol))
        for j in range(1, nrow):
            gram_copy(gram_row, step, row, j - 1, row_at(j), col, 1).start()

    def gram_whole(step):
        for j in range(1, nrow):
            gram_copy(gram_row, step, row_at(j), j - 1, row_at(j), col, 1).wait_recv()
        flat = sum(gram_row[step, r] for r in range(nrow))
        return jnp.concatenate([flat[:, f * vectors : (f + 1) * vectors] for f in range(folds)], axis=0)

    def gram_drain(step):
        for k in range(1, ncol):
            gram_copy(gram_col, step, col, k - 1, row, lax.rem(col + k, ncol), 0).wait_send()
        for j in range(1, nrow):
            gram_copy(gram_row, step, row, j - 1, row_at(j), col, 1).wait_send()

    for k in range(1, nz):
        pass_on(middle, k)
        relay(middle, k - 1)
    relay(middle, nz - 1)
    mixed = jnp.zeros((span, span), jnp.float32)
    acc[...] = jnp.zeros_like(acc)

    def second_row(j):
        sibling_row(middle, j)
        r = row_at(j)
        for s in range(stacks):
            acc[s, :, :span] += jnp.dot(aff[r, s], gs[r], preferred_element_type=jnp.float32)
        return mixed + jnp.dot(upright(gs[r]), gs[r], preferred_element_type=jnp.float32)

    for j in oblique:
        hand_over_row(middle, j)
    for j in [0] + straight:
        mixed = second_row(j)
    for j in oblique:
        mixed = second_row(j)
    gram = sum(
        mixed[s * vectors : (s + 1) * vectors, s * vectors : (s + 1) * vectors] for s in range(stacks)
    )
    first = inverse_factor(gram * (1.0 / total))
    product = sum(acc[s][:, s * vectors : (s + 1) * vectors] for s in range(stacks))
    scaled = lax.dot_general(
        product / degree, first, contract, precision=HIGHEST, preferred_element_type=jnp.float32
    )
    gram_send(0, scaled)
    drain(points)
    drain(start)
    drain(middle)
    gram_across(0)
    second = inverse_factor(gram_whole(0))
    out_ref[...] = lax.dot_general(second, scaled, contract, precision=HIGHEST, preferred_element_type=jnp.float32)
    gram_drain(0)


def solution(mesh):
    nrow, ncol = mesh.shape["row"], mesh.shape["col"]
    nz = ncol // 2

    def step(points, start_vectors):
        rows, features = points.shape
        vectors = start_vectors.shape[1]
        stacks = packing(rows)
        high = rows // stacks
        wide, span = width(stacks, features), width(stacks, vectors)
        dma = pltpu.SemaphoreType.DMA
        gather = [dma((nrow, ncol)), dma((nz,)), dma((nz, nrow)), dma((nrow, nz)), dma((nrow, nz, square_side(nrow)))]
        tall = vectors * vectors // LANES
        return pl.pallas_call(
            functools.partial(kernel, nrow, ncol, rows * nrow * ncol),
            out_shape=jax.ShapeDtypeStruct((vectors, rows), jnp.float32),
            in_specs=[pl.BlockSpec(memory_space=pltpu.VMEM)] * 2,
            out_specs=pl.BlockSpec(memory_space=pltpu.VMEM),
            scratch_shapes=[
                pltpu.VMEM((nrow, ncol * high, wide), jnp.bfloat16),
                pltpu.VMEM((nrow, ncol * high, span), jnp.bfloat16),
                pltpu.VMEM((nrow, ncol * high, span), jnp.bfloat16),
                pltpu.VMEM((nrow, stacks, rows, ncol * high), jnp.bfloat16),
                pltpu.VMEM((stacks, rows, span + LANES), jnp.float32),
                pltpu.VMEM((1, ncol, tall, LANES), jnp.float32),
                pltpu.VMEM((1, nrow, tall, LANES), jnp.float32),
                gather, gather, gather,
                [dma((1, ncol)), dma((1, ncol)), dma((1, nrow)), dma((1, nrow))],
            ],
            compiler_params=pltpu.CompilerParams(
                collective_id=0, has_side_effects=True, vmem_limit_bytes=56 * 1024 * 1024
            ),
        )(points.T, start_vectors.T).T

    return jax.shard_map(
        step,
        mesh=mesh,
        in_specs=(P(("row", "col"), None), P(("row", "col"), None)),
        out_specs=P(("row", "col"), None),
        check_vma=False,
    )
```

profile of v0, /device:TPU:0, one launch (start us, length us, event | category | flops | bytes accessed | tf_op | source)
XLA Modules:
  0.0 53.6 jit_solution(10052674913847566159)
XLA Ops:
  0.0 52.1 %shard_map.28 = f32[32,320]{1,0:T(8,128)} custom-call(bf16[64,320]{1,0:T(8,128)(2,1)} %bitcast.4, bf16[32,320]{1,0:T(8,128)(2,1)} %bitcast.5), custom_call_target="tpu_custom_call" | custom-call | tf_op jit(solution)/shard_map/pallas_call | solution.py:348
  52.1 1.4 %copy.4 = f32[320,32]{0,1:T(8,128)} copy(f32[320,32]{0,1:T(8,128)} %bitcast.3) | data formatting | bytes 81920
where the time goes:
time: 53.8 us; the launch traced here: 53.6 us
  Pallas kernels  52.1 us (97%)
  local copies, waits for them, and re-layouts  1.42 us (3%)
    pallas_call x1, Pallas kernels, step(): pl.pallas_call(functools.partial(kernel, nrow, ncol, rows * nrow * ncol),...  52.1 us
    unnamed x1, local copies, waits for them, and re-layouts  1.42 us

commit v1 on v0

v1 whole, which is shorter than its diff:
```python
import functools

import jax
import jax.numpy as jnp
from jax import lax
from jax.experimental import pallas as pl
from jax.experimental.pallas import tpu as pltpu
from jax.sharding import PartitionSpec as P

KERNEL_SCALE = 5.12
LOG2E = 1.4426950408889634
MESH = pl.DeviceIdType.MESH
HIGHEST = lax.Precision.HIGHEST
LANES = 128
ONES = 16
ROWS_OF = 8


def square_side(count):
    side = 1
    while side * side < count:
        side += 1
    return side if side * side == count else count


def upright(value):
    return value.astype(jnp.float32).T.astype(value.dtype)


def tail_stacks(vectors, rows):
    rest = rows % LANES
    if rest and LANES % rest == 0 and vectors % (LANES // rest * 16) == 0:
        return LANES // rest
    return 1


def packed_rows(vectors, rows):
    full, rest = rows // LANES, rows % LANES
    return full * vectors + (vectors // tail_stacks(vectors, rows) if rest else 0)


def pack(value):
    vectors, rows = value.shape
    full, rest = rows // LANES, rows % LANES
    pieces = [value[:, f * LANES : (f + 1) * LANES] for f in range(full)]
    if rest:
        tail = value[:, full * LANES :]
        stacks = tail_stacks(vectors, rows)
        tall = vectors // stacks
        parts = [tail[s * tall : (s + 1) * tall] for s in range(stacks)]
        spare = LANES - stacks * rest
        if spare:
            parts.append(jnp.zeros((tall, spare), value.dtype))
        pieces.append(jnp.concatenate(parts, axis=1))
    return jnp.concatenate(pieces, axis=0)


def unpack(value, vectors, rows):
    full, rest = rows // LANES, rows % LANES
    pieces = [value[f * vectors : (f + 1) * vectors] for f in range(full)]
    if rest:
        tail = value[full * vectors :]
        stacks = tail_stacks(vectors, rows)
        pieces.append(jnp.concatenate([tail[:, s * rest : (s + 1) * rest] for s in range(stacks)], axis=0))
    return jnp.concatenate(pieces, axis=1)


def inverse_factor(gram):
    size = gram.shape[0]
    down = lax.broadcasted_iota(jnp.int32, (size, size), 0)
    across = lax.broadcasted_iota(jnp.int32, (size, size), 1)
    unit = (down == across).astype(jnp.float32)
    work = jnp.concatenate([gram, unit], axis=1)
    below = lax.broadcasted_iota(jnp.int32, work.shape, 0)
    panel = 8
    for first in range(0, size, panel):
        columns = [jnp.broadcast_to(work[:, k : k + 1], work.shape) for k in range(first, first + panel)]
        for m in range(panel):
            k = first + m
            factor = jnp.where(below > k, columns[m] * (1.0 / columns[m][k : k + 1]), 0.0)
            work = work - factor * work[k : k + 1]
            for later in range(m + 1, panel):
                columns[later] = columns[later] - factor * columns[later][k : k + 1]
    pivots = jnp.sum(work[:, :size] * unit, axis=1, keepdims=True)
    return work[:, size:] * lax.rsqrt(pivots)


def kernel(nrow, ncol, total, pts_ref, vec_ref, out_ref, pair, gp, gv, gx, aff, acc, mine, theirs, gram1, gram2,
           recv_p, recv_v, recv_x, send_g, sems_d):
    row, col = lax.axis_index("row"), lax.axis_index("col")
    nz = ncol // 2
    z, core = col // 2, col % 2
    sibling = (row, z * 2 + (1 - core))
    features, rows = pts_ref.shape
    vectors = vec_ref.shape[0]
    chips = nrow * nz
    both = 2 * rows
    half = rows // 2
    side = square_side(nrow)
    high_row, low_row = row // side, row % side
    lesser = jnp.minimum(z, nz - 1 - z)
    upward = z < nz - 1 - z
    contract = (((1,), (1,)), ((), ()))

    def row_at(j):
        if j == 0:
            return row
        return lax.rem(high_row + j // side, nrow // side) * side + lax.rem(low_row + j % side, side)

    straight = [j for j in range(1, nrow) if j // side == 0 or j % side == 0]
    oblique = [j for j in range(1, nrow) if j // side and j % side]

    def z_at(m):
        if m == 0:
            return z
        q = m - 1
        near = z + (q // 2 + 1) * (1 if q % 2 else -1)
        step = q - lesser + 1
        far = jnp.where(upward, z + step, z - step)
        return jnp.where(q < 2 * lesser, near, far)

    levels = [z_at(m) for m in range(nz)]
    places = [row_at(j) for j in range(nrow)]

    def chip_at(j, m):
        return places[j] * nz + levels[m]

    def block(gather, j, m, to_row, to_z):
        buf, recv, send, routed = gather
        chip = chip_at(j, m)
        return pltpu.make_async_remote_copy(
            src_ref=buf.at[chip], dst_ref=buf.at[chip], send_sem=send_g.at[send], recv_sem=recv.at[chip],
            device_id=(to_row, to_z * 2 + core), device_id_type=MESH,
        )

    def arrived(gather, j, m):
        block(gather, j, m, row, z).wait_recv()

    def spread(gather, m):
        routed = gather[3]
        for j in straight + (oblique if routed else []):
            block(gather, 0, m, places[j], z).start()

    def send_own(gather):
        spread(gather, 0)
        for m in range(1, nz):
            block(gather, 0, 0, row, levels[m]).start()

    def pass_on(gather, m):
        arrived(gather, 0, m)
        spread(gather, m)

    def relay(gather, m):
        routed = gather[3]
        for j in straight:
            arrived(gather, j, m)
            if routed:
                continue
            if j // side == 0 and m % 2 == 0:
                targets = [d * side for d in range(1, nrow // side)]
            elif j % side == 0 and m % 2 == 1:
                targets = range(1, side)
            else:
                targets = []
            for t in targets:
                block(gather, j, m, places[t], z).start()

    def drain(gather):
        buf, recv, send, routed = gather
        sent = buf.at[pl.ds(0, chips - 1)]
        pltpu.make_async_remote_copy(
            src_ref=sent, dst_ref=sent, send_sem=send_g.at[send], recv_sem=recv.at[0],
            device_id=(row, col), device_id_type=MESH,
        ).wait_send()

    def swap(src, dst, n):
        return pltpu.make_async_remote_copy(
            src_ref=src, dst_ref=dst, send_sem=sems_d.at[2 * n], recv_sem=sems_d.at[2 * n + 1],
            device_id=sibling, device_id_type=MESH,
        )

    points = (gp, recv_p, 0, False)
    start = (gv, recv_v, 1, False)
    middle = (gx, recv_x, 2, True)

    barrier = pltpu.get_barrier_semaphore()
    for j in range(1, nrow):
        pl.semaphore_signal(barrier, inc=1, device_id=(places[j], col), device_id_type=MESH)
    for m in range(1, nz):
        pl.semaphore_signal(barrier, inc=1, device_id=(row, levels[m] * 2 + core), device_id_type=MESH)
    pl.semaphore_signal(barrier, inc=1, device_id=sibling, device_id_type=MESH)

    own = chip_at(0, 0)
    x = upright(pts_ref[...])
    gp[own] = jnp.concatenate([x[:half], x[half:]], axis=1)
    gv[own] = pack(vec_ref[...])
    with jax.named_scope("barrier"):
        pl.semaphore_wait(barrier, nrow + nz - 1)

    swap_points = swap(pts_ref, pair, 0)
    swap_points.start()
    send_own(points)
    send_own(start)

    rate = -KERNEL_SCALE / features * LOG2E
    with jax.named_scope("prep"):
        swap_points.wait()
        ours, other = pts_ref[...].astype(jnp.float32), pair[...].astype(jnp.float32)
        first_core = core == 0
        lane_points = jnp.concatenate(
            [jnp.where(first_core, ours, other), jnp.where(first_core, other, ours)], axis=1
        )
        here = jnp.sum(lane_points * lane_points, axis=0, keepdims=True) * rate
        lane_points = lane_points.astype(jnp.bfloat16)
        blank = jnp.zeros_like(lane_points)
        right = [
            jnp.concatenate([lane_points, blank], axis=0),
            jnp.concatenate([blank, lane_points], axis=0),
        ]
        lane = lax.broadcasted_iota(jnp.int32, (2 * LANES, 2 * LANES), 1)
        down = lax.broadcasted_iota(jnp.int32, (2 * LANES, 2 * LANES), 0)
        picks = (lax.rem(down, LANES) // features == lane // LANES).astype(jnp.bfloat16)

    def weights(j, m):
        left = gp[chip_at(j, m)]
        wide = left.astype(jnp.float32)
        square = wide * wide
        upper = square.astype(jnp.bfloat16)
        lower = (square - upper.astype(jnp.float32)).astype(jnp.bfloat16)
        there = jnp.dot(
            jnp.concatenate([upper, lower], axis=1), picks, preferred_element_type=jnp.float32
        ) * rate
        for t in range(2):
            cross = jnp.dot(left, right[t], preferred_element_type=jnp.float32)
            tile = there[:, t * LANES : (t + 1) * LANES]
            tiles = jnp.concatenate([tile] * (-(-both // LANES)), axis=1)[:, :both]
            power = (cross * (-2.0 * rate) + tiles) + here
            aff[j * nz + m, t * half : (t + 1) * half, :] = jnp.exp2(power).astype(jnp.bfloat16)

    counter = jnp.ones((ONES, rows), jnp.bfloat16)

    def first_product(blocks):
        part = 0.0
        for j, m in blocks:
            panel = jnp.concatenate([unpack(gv[chip_at(j, m)], vectors, rows), counter], axis=0)
            part = part + jnp.dot(panel, aff[j * nz + m], preferred_element_type=jnp.float32)
        return part

    with jax.named_scope("w_own"):
        weights(0, 0)
    for m in range(1, nz):
        with jax.named_scope(f"pass_p{m}"):
            pass_on(points, m)
            relay(points, m - 1)
        with jax.named_scope(f"w{m}"):
            weights(0, m)
            for j in straight:
                weights(j, m - 1)
        with jax.named_scope(f"pass_v{m}"):
            pass_on(start, m)
            relay(start, m - 1)
        if m > 1:
            for j in oblique:
                with jax.named_scope(f"wait_o{m - 2}"):
                    arrived(points, j, m - 2)
                with jax.named_scope(f"wo{m - 2}"):
                    weights(j, m - 2)
    with jax.named_scope("relay_p_last"):
        relay(points, nz - 1)
    with jax.named_scope("w_last"):
        for j in straight:
            weights(j, nz - 1)
    with jax.named_scope("first_a"):
        acc[...] = first_product([(0, m) for m in range(nz)] + [(j, m) for j in straight for m in range(nz - 1)])
    with jax.named_scope("relay_v_last"):
        relay(start, nz - 1)
    with jax.named_scope("first_b"):
        acc[...] += first_product([(j, nz - 1) for j in straight])
    for j in oblique:
        for m in range(max(0, nz - 2), nz):
            with jax.named_scope(f"wait_o{m}"):
                arrived(points, j, m)
            with jax.named_scope(f"wo{m}"):
                weights(j, m)
    with jax.named_scope("wait_vo"):
        for j in oblique:
            for m in range(nz):
                arrived(start, j, m)
    with jax.named_scope("first_c"):
        mine[...] = (acc[...] + first_product([(j, m) for j in oblique for m in range(nz)]))[: vectors + ROWS_OF]
    swap_first = swap(mine, theirs.at[0], 1)
    swap_first.start()
    with jax.named_scope("swap1"):
        swap_first.wait()

    with jax.named_scope("scale_send"):
        whole = mine[...] + theirs[0]
        degree = whole[vectors : vectors + 1]
        scaled = whole[:vectors] / degree
        ours = jnp.where(first_core, scaled[:, :rows], scaled[:, rows:])
        gx[own] = pack(ours.astype(jnp.bfloat16))
        send_own(middle)

    def second_product(blocks):
        part, cross = 0.0, 0.0
        for j, m in blocks:
            panel = unpack(gx[chip_at(j, m)], vectors, rows)
            part = part + jnp.dot(panel, aff[j * nz + m], preferred_element_type=jnp.float32)
            cross = cross + lax.dot_general(panel, panel, contract, preferred_element_type=jnp.float32)
        return part, cross

    with jax.named_scope("second_own"):
        part, cross = second_product([(0, 0)])
        acc[:vectors] = part
    for m in range(1, nz):
        with jax.named_scope(f"pass_x{m}"):
            pass_on(middle, m)
            relay(middle, m - 1)
        with jax.named_scope(f"second{m}"):
            part, more = second_product([(0, m)] + [(j, m - 1) for j in straight])
            acc[:vectors] += part
            cross = cross + more
    with jax.named_scope("relay_x_last"):
        relay(middle, nz - 1)
    with jax.named_scope("second_last"):
        part, more = second_product([(j, nz - 1) for j in straight])
        acc[:vectors] += part
        cross = cross + more
    with jax.named_scope("wait_xo"):
        for j in oblique:
            for m in range(nz):
                arrived(middle, j, m)
    with jax.named_scope("second_o"):
        part, more = second_product([(j, m) for j in oblique for m in range(nz)])
        gram1[0] = cross + more
        swap_gram = swap(gram1.at[0], gram1.at[1], 2)
        swap_gram.start()
        mine[:vectors] = acc[:vectors] + part
        swap_second = swap(mine.at[pl.ds(0, vectors)], theirs.at[1, pl.ds(0, vectors)], 3)
        swap_second.start()
    with jax.named_scope("swap_gram"):
        swap_gram.wait()
    with jax.named_scope("factor1"):
        first = inverse_factor((gram1[0] + gram1[1]) * (1.0 / total))
    with jax.named_scope("swap2"):
        swap_second.wait()
    folds = LANES // vectors
    tall = vectors // folds
    with jax.named_scope("gram2"):
        ratio = (mine[:vectors] + theirs[1, :vectors]) / degree
        scaled = jnp.dot(first, ratio, precision=HIGHEST, preferred_element_type=jnp.float32)
        part = lax.dot_general(
            scaled, scaled, contract, precision=HIGHEST, preferred_element_type=jnp.float32
        ) * (1.0 / total)
        gram2[own] = jnp.concatenate([part[f * tall : (f + 1) * tall] for f in range(folds)], axis=1)

    def gram_copy(j, m, to_row, to_z):
        chip = chip_at(j, m)
        return pltpu.make_async_remote_copy(
            src_ref=gram2.at[chip], dst_ref=gram2.at[chip], send_sem=sems_d.at[8], recv_sem=sems_d.at[9],
            device_id=(to_row, to_z * 2 + core), device_id_type=MESH,
        )

    with jax.named_scope("gram_send"):
        for m in reversed(range(nz)):
            for j in reversed(range(nrow)):
                if j or m:
                    gram_copy(0, 0, places[j], levels[m]).start()
        ours = jnp.where(first_core, scaled[:, :rows], scaled[:, rows:])
        drain(points)
        drain(start)
        drain(middle)
        sent = gram2.at[pl.ds(0, chips - 1)]
    with jax.named_scope("gram_wait"):
        pltpu.make_async_remote_copy(
            src_ref=sent, dst_ref=sent, send_sem=sems_d.at[8], recv_sem=sems_d.at[9],
            device_id=(row, col), device_id_type=MESH,
        ).wait()
    with jax.named_scope("factor2"):
        flat = jnp.sum(gram2[...], axis=0)
        gram = jnp.concatenate([flat[:, f * vectors : (f + 1) * vectors] for f in range(folds)], axis=0)
        second = inverse_factor(gram)
    with jax.named_scope("out"):
        out_ref[...] = jnp.dot(second, ours, precision=HIGHEST, preferred_element_type=jnp.float32)


def solution(mesh):
    nrow, ncol = mesh.shape["row"], mesh.shape["col"]
    nz = ncol // 2
    chips = nrow * nz

    def step(points, start_vectors):
        rows, features = points.shape
        vectors = start_vectors.shape[1]
        high = packed_rows(vectors, rows)
        dma = pltpu.SemaphoreType.DMA
        return pl.pallas_call(
            functools.partial(kernel, nrow, ncol, rows * nrow * ncol),
            out_shape=jax.ShapeDtypeStruct((vectors, rows), jnp.float32),
            in_specs=[pl.BlockSpec(memory_space=pltpu.VMEM)] * 2,
            out_specs=pl.BlockSpec(memory_space=pltpu.VMEM),
            scratch_shapes=[
                pltpu.VMEM((features, rows), jnp.bfloat16),
                pltpu.VMEM((chips, rows // 2, 2 * features), jnp.bfloat16),
                pltpu.VMEM((chips, high, LANES), jnp.bfloat16),
                pltpu.VMEM((chips, high, LANES), jnp.bfloat16),
                pltpu.VMEM((chips, rows, 2 * rows), jnp.bfloat16),
                pltpu.VMEM((vectors + ONES, 2 * rows), jnp.float32),
                pltpu.VMEM((vectors + ROWS_OF, 2 * rows), jnp.float32),
                pltpu.VMEM((2, vectors + ROWS_OF, 2 * rows), jnp.float32),
                pltpu.VMEM((2, vectors, vectors), jnp.float32),
                pltpu.VMEM((chips, vectors * vectors // LANES, LANES), jnp.float32),
                dma((chips,)), dma((chips,)), dma((chips,)), dma((3,)), dma((10,)),
            ],
            compiler_params=pltpu.CompilerParams(
                collective_id=0, has_side_effects=True, vmem_limit_bytes=56 * 1024 * 1024
            ),
        )(points.T, start_vectors.T).T

    return jax.shard_map(
        step,
        mesh=mesh,
        in_specs=(P(("row", "col"), None), P(("row", "col"), None)),
        out_specs=P(("row", "col"), None),
        check_vma=False,
    )
```

time: 53.8 us -> 45.6 us (0.85)
  Pallas kernels: 52.1 us -> 44 us
    pallas_call x1, Pallas kernels: 52.1 us -> 44 us  [step(): pl.pallas_call(functools.partial(kernel, nrow, ncol, rows * nrow * ncol),...]
where the time goes in v1:
time: 45.6 us; the launch traced here: 45.4 us
  Pallas kernels  44 us (96%)
  local copies, waits for them, and re-layouts  1.42 us (3%)
    pallas_call x1, Pallas kernels, step(): pl.pallas_call(functools.partial(kernel, nrow, ncol, rows * nrow * ncol),...  44 us
    unnamed x1, local copies, waits for them, and re-layouts  1.42 us

profile of v1, /device:TPU:0, one launch (start us, length us, event | category | flops | bytes accessed | tf_op | source)
XLA Modules:
  0.0 45.4 jit_solution(6890522211128129416)
XLA Ops:
  0.0 44.0 %shard_map.28 = f32[32,320]{1,0:T(8,128)} custom-call(bf16[64,320]{1,0:T(8,128)(2,1)} %bitcast.4, bf16[32,320]{1,0:T(8,128)(2,1)} %bitcast.5), custom_call_target="tpu_custom_call" | custom-call | tf_op jit(solution)/shard_map/pallas_call | solution.py:397
  44.0 1.4 %copy.4 = f32[320,32]{0,1:T(8,128)} copy(f32[320,32]{0,1:T(8,128)} %bitcast.3) | data formatting | bytes 81920
